TPU v7x, 32 devices: a whole 2x2x4 slice. The times are simulated.
32 devices in a mesh: ctg: 8 (over y, x, core), br: 4 (over z).
Axes of the slice: x: 2, y: 2, z: 4, core: 2. Of those that a mesh axis runs over, the one named last changes fastest.
Arguments:
- base_vm: float32 [10240], P(('ctg', 'br')), may hold values from 0.95 to 1.05
- base_va: float32 [10240], P(('ctg', 'br')), may hold values from -0.6 to 0.6
- delta_state: float32 [64, 2, 10240], P('ctg', None, 'br'), may hold values from -0.18 to 0.18
- multipliers: float32 [64, 2, 10240], P('ctg', None, 'br'), may hold values from -6 to 6
- net_inj: float32 [64, 2, 10240], P('ctg', None, 'br'), may hold values from -6 to 6
- ang_grad: float32 [64, 10240], P('ctg', 'br'), may hold values from -6 to 6
- from_bus: int32 [13312], P('br'), may hold values from 0 to 10239
- to_bus: int32 [13312], P('br'), may hold values from 0 to 10239
- status: int32 [64, 13312], P('ctg', 'br'), may hold values 0 or 1
- conduct: float32 [13312], P('br'), may hold values from 1 to 5
- suscept: float32 [13312], P('br'), may hold values from -15 to -5
- charging: float32 [13312], P('br'), may hold values from 0.1 to 0.6
- rating: float32 [13312], P('br'), may hold values from 1 to 3
- slack: float32 [64, 13312], P('ctg', 'br'), may hold values from 0.05 to 2
- zdual: float32 [64, 13312], P('ctg', 'br'), may hold values from 0.05 to 2
Outputs:
- mismatch: float32 [64, 2, 10240], P('ctg', None, 'br')
- dual_res: float32 [64, 10240], P('ctg', 'br')
- limit_res: float32 [64, 13312], P('ctg', 'br')
- ctg_norms: float32 [64, 4], P('ctg')
- total_norms: float32 [4], replicated
All inputs are finite; a program needn't handle non-finite values. No bound on the sum of `status` on one device may be relied on, other than what follows from the above.
Results may differ from a plain program's by a relative error of at most 0.0003.
Values sent between devices are 32-bit elements; how exact they have to be, the bound alone decides.
A program may use at most 64 MiB of HBM per device.

v0:
```python
import math
import jax
import jax.numpy as jnp
from jax import lax
from jax.sharding import PartitionSpec as P


def block_size(span_total, other_side):
    limit = max(128, (1 << 23) // other_side)
    power = 1 << limit.bit_length() - 1
    return math.gcd(span_total, min(1024, power))


def select_cols(values, index_list):
    row_count, bus_count = values.shape
    col_count = index_list.shape[0]
    span_cols = block_size(bus_count, col_count)
    block_count = bus_count // span_cols
    tiles = values.reshape(row_count, block_count, span_cols).transpose(1, 0, 2)

    def add_block(running, item):
        segment, number = item
        labels = number * span_cols + lax.iota(jnp.int32, span_cols)
        onehot = (labels[:, None] == index_list[None, :]).astype(jnp.float32)
        running = running + jnp.dot(
            segment, onehot, precision=lax.Precision.HIGHEST, preferred_element_type=jnp.float32
        )
        return (running, None)

    start_zero = jnp.zeros((row_count, col_count), jnp.float32)
    numbers = jnp.arange(block_count, dtype=jnp.int32)
    result, _ = lax.scan(add_block, start_zero, (tiles, numbers))
    return result


def spread_rows(values, index_list, bus_count):
    row_count, col_count = values.shape
    span_cols = block_size(bus_count, col_count)
    block_count = bus_count // span_cols

    def one_block(carry, number):
        labels = number * span_cols + lax.iota(jnp.int32, span_cols)
        onehot = (index_list[:, None] == labels[None, :]).astype(jnp.float32)
        piece_sum = jnp.dot(
            values, onehot, precision=lax.Precision.HIGHEST, preferred_element_type=jnp.float32
        )
        return (carry, piece_sum)

    numbers = jnp.arange(block_count, dtype=jnp.int32)
    _, pieces = lax.scan(one_block, jnp.int32(0), numbers)
    return pieces.transpose(1, 0, 2).reshape(row_count, bus_count)


def branch_flows(
    volt_mag, volt_ang, mult_p, mult_q, from_idx, to_idx, conduct, suscept, charging, in_service
):
    scen_count = volt_mag.shape[0]
    stacked = jnp.concatenate([volt_mag, volt_ang, mult_p, mult_q], 0)
    at_from_end = select_cols(stacked, from_idx)
    at_to_end = select_cols(stacked, to_idx)
    volt_from = at_from_end[:scen_count]
    volt_to = at_to_end[:scen_count]
    angle_diff = at_from_end[scen_count : 2 * scen_count] - at_to_end[scen_count : 2 * scen_count]
    mp_from = at_from_end[2 * scen_count : 3 * scen_count]
    mq_from = at_from_end[3 * scen_count :]
    mp_to = at_to_end[2 * scen_count : 3 * scen_count]
    mq_to = at_to_end[3 * scen_count :]
    cos_diff = jnp.cos(angle_diff)
    sin_diff = jnp.sin(angle_diff)
    volt_prod = volt_from * volt_to
    p_from = conduct * volt_from * volt_from - volt_prod * (conduct * cos_diff + suscept * sin_diff)
    q_from = -(suscept + charging) * volt_from * volt_from - volt_prod * (
        conduct * sin_diff - suscept * cos_diff
    )
    p_to = conduct * volt_to * volt_to - volt_prod * (conduct * cos_diff - suscept * sin_diff)
    q_to = -(suscept + charging) * volt_to * volt_to + volt_prod * (
        conduct * sin_diff + suscept * cos_diff
    )
    flow_dual = volt_prod * (
        mp_from * (conduct * sin_diff - suscept * cos_diff)
        - mq_from * (conduct * cos_diff + suscept * sin_diff)
        + mp_to * (conduct * sin_diff + suscept * cos_diff)
        + mq_to * (conduct * cos_diff - suscept * sin_diff)
    )
    at_from = jnp.stack([p_from, q_from, flow_dual], 1) * in_service[:, None, :]
    at_to = jnp.stack([p_to, q_to, -flow_dual], 1) * in_service[:, None, :]
    return (at_from, at_to)


def sum_at_buses(from_vals, to_vals, from_idx, to_idx, offset, bus_count):
    scen_count = from_vals.shape[0]
    both_vals = jnp.concatenate([from_vals, to_vals], 2).reshape(scen_count * 3, -1)
    both_idx = jnp.concatenate([from_idx, to_idx], 0) - offset
    summed = spread_rows(both_vals, both_idx, bus_count)
    return summed.reshape(scen_count, 3, bus_count)


def per_device(
    base_vm,
    base_va,
    delta_state,
    multipliers,
    net_inj,
    ang_grad,
    from_bus,
    to_bus,
    status,
    conduct,
    suscept,
    charging,
    rating,
    slack,
    zdual,
):
    full_vm, full_va = (
        lax.all_gather(base_vm, ("ctg", "br"), axis=0, tiled=True),
        lax.all_gather(base_va, ("ctg", "br"), axis=0, tiled=True),
    )
    shifts, duals_all = (
        lax.all_gather(delta_state, "br", axis=2, tiled=True),
        lax.all_gather(multipliers, "br", axis=2, tiled=True),
    )
    volt_mag = full_vm[None, :] + shifts[:, 0]
    volt_ang = full_va[None, :] + shifts[:, 1]
    own_buses = delta_state.shape[2]
    offset = lax.axis_index("br") * own_buses
    in_service = status.astype(jnp.float32)
    at_from, at_to = branch_flows(
        volt_mag,
        volt_ang,
        duals_all[:, 0],
        duals_all[:, 1],
        from_bus,
        to_bus,
        conduct,
        suscept,
        charging,
        in_service,
    )
    limit_res = in_service * (
        at_from[:, 0] * at_from[:, 0] + at_from[:, 1] * at_from[:, 1] + slack - rating * rating
    )
    complement = in_service * (zdual * slack - 0.01)
    limit_part = jnp.sum(limit_res * limit_res, axis=1)
    comp_part = jnp.sum(complement * complement, axis=1)
    limit_sq, comp_sq = lax.psum((limit_part, comp_part), "br")
    every_from, every_to = (
        lax.all_gather(at_from, "br", axis=2, tiled=True),
        lax.all_gather(at_to, "br", axis=2, tiled=True),
    )
    ends_from, ends_to = (
        lax.all_gather(from_bus, "br", axis=0, tiled=True),
        lax.all_gather(to_bus, "br", axis=0, tiled=True),
    )
    summed = sum_at_buses(every_from, every_to, ends_from, ends_to, offset, own_buses)
    mismatch = summed[:, :2] - net_inj
    dual_res = summed[:, 2] + ang_grad
    mis_part = jnp.sum(mismatch * mismatch, axis=(1, 2))
    dual_part = jnp.sum(dual_res * dual_res, axis=1)
    mis_sq, dual_sq = lax.psum((mis_part, dual_part), "br")
    squares = jnp.stack([mis_sq, dual_sq, limit_sq, comp_sq], 1)
    ctg_norms = jnp.sqrt(squares)
    totals = lax.psum(jnp.sum(squares, axis=0), "ctg")
    total_norms = jnp.sqrt(totals / (delta_state.shape[0] * lax.axis_size("ctg")))
    return (mismatch, dual_res, limit_res, ctg_norms, total_norms)


def solution(mesh):
    placed = (
        P(("ctg", "br")),
        P(("ctg", "br")),
        P("ctg", None, "br"),
        P("ctg", None, "br"),
        P("ctg", None, "br"),
        P("ctg", "br"),
        P("br"),
        P("br"),
        P("ctg", "br"),
        P("br"),
        P("br"),
        P("br"),
        P("br"),
        P("ctg", "br"),
        P("ctg", "br"),
    )
    return jax.shard_map(
        per_device,
        mesh=mesh,
        in_specs=placed,
        out_specs=(P("ctg", None, "br"), P("ctg", "br"), P("ctg", "br"), P("ctg", None), P()),
        check_vma=False,
    )
```

profile of v0, /device:TPU:0, one launch (start us, length us, event | category | flops | bytes accessed | tf_op | source)
XLA Modules:
  0.0 480.9 jit_solution(18033969470416528919)
XLA Ops:
  7.3 0.9 dynamic-update-slice
  8.2 0.9 dynamic-update-slice.1
  9.1 0.6 copy-done.3
  9.8 1.0 copy.26
  10.7 19.8 %all_gather.27 = f32[8,2,10240]{2,0,1:T(8,128)S(1)} all-gather(f32[8,2,2560]{2,0,1:T(8,128)S(1)} %copy.26), channel_id=1, replica_groups=mesh['ctg'=8,'br'=4] {'br'}, dimensions={2}, use_global_device_ids=true | all-gather | bytes 819200 | tf_op jit(solution)/shard_map/all_gather | solution.py:120
  30.6 16.5 %all_gather.29 = f32[8,2,10240]{2,0,1:T(8,128)S(1)} all-gather(f32[8,2,2560]{2,0,1:T(8,128)S(1)} %copy.27), channel_id=1, replica_groups=mesh['ctg'=8,'br'=4] {'br'}, dimensions={2}, use_global_device_ids=true | all-gather | bytes 819200 | tf_op jit(solution)/shard_map/all_gather | solution.py:121
  47.3 92.3 %all-reduce.6.cloned.1.call-done = (f32[10240]{0:T(1024)}, f32[10240]{0:T(1024)}) async-done(((f32[10240]{0:T(1024)}, f32[10240]{0:T(1024)}), (f32[10240]{0:T(1024)}, f32[10240]{0:T(1024)})) %all-reduce.6.cloned.1.call-update) | async-done | bytes 81936
  139.6 0.8 add.111
  140.4 0.8 add.114
  141.4 57.5 %while.34 = (s32[]{:T(128)}, f32[32,3328]{1,0:T(8,128)S(1)}, f32[10,32,1024]{2,1,0:T(8,128)S(1)}, s32[10]{0:T(128)S(1)}, s32[3328]{0:T(1024)S(1)}, /*index=5*/s32[]{:T(128)}, s32[1]{0:T(128)}, s32[]{:T(128)}) while((s32[]{:T(128)}, f32[32,3328]{1,0:T(8,128)S(1)}, f32[10,32,1024]{2,1,0:T(8,128)S(1)}, s32[10]{0:T(128)S(1)}, ...), condition=%wide.region_3.4_spmd.clone, body=%wide.region_2.3_spmd.clone.sunk | while | flops 1312244736 | bytes 1007743 | solution.py:32
  142.7 4.5 fusion.70
  147.2 0.6 dynamic_slice.38
  148.4 4.5 fusion.70
  152.9 0.6 dynamic_slice.38
  154.2 4.5 fusion.70
  159.9 4.5 fusion.70
  164.4 0.6 dynamic_slice.38
  165.7 4.5 fusion.70
  170.2 0.6 dynamic_slice.38
  171.4 4.5 fusion.70
  175.9 0.6 dynamic_slice.38
  177.2 4.5 fusion.70
  181.7 0.6 dynamic_slice.38
  182.9 4.5 fusion.70
  188.7 4.5 fusion.70
  194.4 4.5 fusion.70
  199.0 57.5 %while.33 = (s32[]{:T(128)}, f32[32,3328]{1,0:T(8,128)S(1)}, f32[10,32,1024]{2,1,0:T(8,128)S(1)}, s32[10]{0:T(128)S(1)}, s32[3328]{0:T(1024)S(1)}, /*index=5*/s32[]{:T(128)}, s32[1]{0:T(128)}, s32[]{:T(128)}) while((s32[]{:T(128)}, f32[32,3328]{1,0:T(8,128)S(1)}, f32[10,32,1024]{2,1,0:T(8,128)S(1)}, s32[10]{0:T(128)S(1)}, ...), condition=%wide.region_1.2_spmd.clone, body=%wide.region_0.1_spmd.clone.sunk | while | flops 1312244736 | bytes 1007743 | solution.py:32
  200.2 4.5 fusion.67
  206.0 4.5 fusion.67
  211.7 4.5 fusion.67
  217.5 4.5 fusion.67
  223.2 4.5 fusion.67
  229.0 4.5 fusion.67
  234.7 4.5 fusion.67
  240.5 4.5 fusion.67
  246.2 4.5 fusion.67
  252.0 4.5 fusion.67
  257.0 0.9 maximum_multiply_fusion
  258.0 0.7 all-gather.7.cloned.1.call-update
  258.8 14.7 %all-gather = s32[4,1,3328]{2,1,0:T(1,128)S(1)} all-gather(s32[1,1,3328]{2,1,0:T(1,128)S(1)} %reshape.69), channel_id=1, replica_groups=mesh['ctg'=8,'br'=4] {'br'}, dimensions={0}, use_global_device_ids=true | all-gather | bytes 66560 | tf_op jit(solution)/shard_map/all_gather | solution.py:152
  273.5 14.6 %all-gather.1 = s32[4,1,3328]{2,1,0:T(1,128)S(1)} all-gather(s32[1,1,3328]{2,1,0:T(1,128)S(1)} %reshape.71), channel_id=1, replica_groups=mesh['ctg'=8,'br'=4] {'br'}, dimensions={0}, use_global_device_ids=true | all-gather | bytes 66560 | tf_op jit(solution)/shard_map/all_gather | solution.py:153
  288.1 1.8 multiply_reduce_fusion.2
  289.9 3.3 all-gather.5.cloned.1.call-done
  293.2 32.5 %all-gather.7.cloned.1.call-done = f32[8,3,13312]{2,0,1:T(8,128)} async-done(((f32[8,3,3328]{2,0,1:T(8,128)}), f32[8,3,13312]{2,0,1:T(8,128)}) %all-gather.7.cloned.1.call-update) | async-done | bytes 1277968 | tf_op jit(solution)/shard_map/all_gather | solution.py:149
  325.7 1.9 pad_maximum_fusion
  327.6 1.8 copy.28
  329.4 2.8 reshape.64
  332.1 116.5 %while.32 = (s32[]{:T(128)}, f32[10,24,256]{2,1,0:T(8,128)}, s32[26624]{0:T(1024)S(1)}, s32[10]{0:T(128)S(1)}, f32[24,26624]{1,0:T(8,128)}, /*index=5*/s32[]{:T(128)}, s32[1]{0:T(128)}) while((s32[]{:T(128)}, f32[10,24,256]{2,1,0:T(8,128)}, s32[26624]{0:T(1024)S(1)}, s32[10]{0:T(128)S(1)}, f32[24,26624]{1,0:T(8,128)}, /*index=5*/s32[]{:T(128)}, ...), condition=%wide.region_5.6_spmd, body=%wide.region_4.5_spmd.sunk | while | flops 1969750272 | bytes 2689641 | solution.py:50
  333.4 10.4 %fusion.64 = f32[10,24,256]{2,1,0:T(8,128)} fusion(f32[10,24,256]{2,1,0:T(8,128)} %get-tuple-element.341, s32[]{:T(128)} %get-tuple-element.340, f32[24,26624]{1,0:T(8,128)} %get-tuple-element.351, s32[256]{0:T(256)S(1)} %iota_add_fusion.6, s32[26624]{0:T(1024)S(1)} %get-tuple-element.349), kind=kOutput, calls=%fused_computation.5.clone.1 | convolution fusion | flops 1969750016 | bytes 2688512 | tf_op jit(solution)/shard_map/while/body/eval_jaxpr/dot_general | solution.py:44
  345.0 10.4 %fusion.64 = f32[10,24,256]{2,1,0:T(8,128)} fusion(f32[10,24,256]{2,1,0:T(8,128)} %get-tuple-element.341, s32[]{:T(128)} %get-tuple-element.340, f32[24,26624]{1,0:T(8,128)} %get-tuple-element.351, s32[256]{0:T(256)S(1)} %iota_add_fusion.6, s32[26624]{0:T(1024)S(1)} %get-tuple-element.349), kind=kOutput, calls=%fused_computation.5.clone.1 | convolution fusion | flops 1969750016 | bytes 2688512 | tf_op jit(solution)/shard_map/while/body/eval_jaxpr/dot_general | solution.py:44
  356.7 10.4 %fusion.64 = f32[10,24,256]{2,1,0:T(8,128)} fusion(f32[10,24,256]{2,1,0:T(8,128)} %get-tuple-element.341, s32[]{:T(128)} %get-tuple-element.340, f32[24,26624]{1,0:T(8,128)} %get-tuple-element.351, s32[256]{0:T(256)S(1)} %iota_add_fusion.6, s32[26624]{0:T(1024)S(1)} %get-tuple-element.349), kind=kOutput, calls=%fused_computation.5.clone.1 | convolution fusion | flops 1969750016 | bytes 2688512 | tf_op jit(solution)/shard_map/while/body/eval_jaxpr/dot_general | solution.py:44
  368.3 10.4 %fusion.64 = f32[10,24,256]{2,1,0:T(8,128)} fusion(f32[10,24,256]{2,1,0:T(8,128)} %get-tuple-element.341, s32[]{:T(128)} %get-tuple-element.340, f32[24,26624]{1,0:T(8,128)} %get-tuple-element.351, s32[256]{0:T(256)S(1)} %iota_add_fusion.6, s32[26624]{0:T(1024)S(1)} %get-tuple-element.349), kind=kOutput, calls=%fused_computation.5.clone.1 | convolution fusion | flops 1969750016 | bytes 2688512 | tf_op jit(solution)/shard_map/while/body/eval_jaxpr/dot_general | solution.py:44
  380.0 10.4 %fusion.64 = f32[10,24,256]{2,1,0:T(8,128)} fusion(f32[10,24,256]{2,1,0:T(8,128)} %get-tuple-element.341, s32[]{:T(128)} %get-tuple-element.340, f32[24,26624]{1,0:T(8,128)} %get-tuple-element.351, s32[256]{0:T(256)S(1)} %iota_add_fusion.6, s32[26624]{0:T(1024)S(1)} %get-tuple-element.349), kind=kOutput, calls=%fused_computation.5.clone.1 | convolution fusion | flops 1969750016 | bytes 2688512 | tf_op jit(solution)/shard_map/while/body/eval_jaxpr/dot_general | solution.py:44
  391.6 10.4 %fusion.64 = f32[10,24,256]{2,1,0:T(8,128)} fusion(f32[10,24,256]{2,1,0:T(8,128)} %get-tuple-element.341, s32[]{:T(128)} %get-tuple-element.340, f32[24,26624]{1,0:T(8,128)} %get-tuple-element.351, s32[256]{0:T(256)S(1)} %iota_add_fusion.6, s32[26624]{0:T(1024)S(1)} %get-tuple-element.349), kind=kOutput, calls=%fused_computation.5.clone.1 | convolution fusion | flops 1969750016 | bytes 2688512 | tf_op jit(solution)/shard_map/while/body/eval_jaxpr/dot_general | solution.py:44
  403.2 10.4 %fusion.64 = f32[10,24,256]{2,1,0:T(8,128)} fusion(f32[10,24,256]{2,1,0:T(8,128)} %get-tuple-element.341, s32[]{:T(128)} %get-tuple-element.340, f32[24,26624]{1,0:T(8,128)} %get-tuple-element.351, s32[256]{0:T(256)S(1)} %iota_add_fusion.6, s32[26624]{0:T(1024)S(1)} %get-tuple-element.349), kind=kOutput, calls=%fused_computation.5.clone.1 | convolution fusion | flops 1969750016 | bytes 2688512 | tf_op jit(solution)/shard_map/while/body/eval_jaxpr/dot_general | solution.py:44
  414.9 10.4 %fusion.64 = f32[10,24,256]{2,1,0:T(8,128)} fusion(f32[10,24,256]{2,1,0:T(8,128)} %get-tuple-element.341, s32[]{:T(128)} %get-tuple-element.340, f32[24,26624]{1,0:T(8,128)} %get-tuple-element.351, s32[256]{0:T(256)S(1)} %iota_add_fusion.6, s32[26624]{0:T(1024)S(1)} %get-tuple-element.349), kind=kOutput, calls=%fused_computation.5.clone.1 | convolution fusion | flops 1969750016 | bytes 2688512 | tf_op jit(solution)/shard_map/while/body/eval_jaxpr/dot_general | solution.py:44
  426.6 10.4 %fusion.64 = f32[10,24,256]{2,1,0:T(8,128)} fusion(f32[10,24,256]{2,1,0:T(8,128)} %get-tuple-element.341, s32[]{:T(128)} %get-tuple-element.340, f32[24,26624]{1,0:T(8,128)} %get-tuple-element.351, s32[256]{0:T(256)S(1)} %iota_add_fusion.6, s32[26624]{0:T(1024)S(1)} %get-tuple-element.349), kind=kOutput, calls=%fused_computation.5.clone.1 | convolution fusion | flops 1969750016 | bytes 2688512 | tf_op jit(solution)/shard_map/while/body/eval_jaxpr/dot_general | solution.py:44
  438.2 10.4 %fusion.64 = f32[10,24,256]{2,1,0:T(8,128)} fusion(f32[10,24,256]{2,1,0:T(8,128)} %get-tuple-element.341, s32[]{:T(128)} %get-tuple-element.340, f32[24,26624]{1,0:T(8,128)} %get-tuple-element.351, s32[256]{0:T(256)S(1)} %iota_add_fusion.6, s32[26624]{0:T(1024)S(1)} %get-tuple-element.349), kind=kOutput, calls=%fused_computation.5.clone.1 | convolution fusion | flops 1969750016 | bytes 2688512 | tf_op jit(solution)/shard_map/while/body/eval_jaxpr/dot_general | solution.py:44
  448.6 1.0 copy.29
  449.9 0.8 multiply_reduce_fusion
  450.7 0.8 multiply_reduce_fusion.3
  451.4 10.0 %all-reduce.3 = (f32[8,1]{0,1:T(1,128)S(1)}, f32[8,1]{0,1:T(1,128)S(1)}, f32[8,1]{0,1:T(1,128)S(1)}, f32[8,1]{0,1:T(1,128)S(1)}) all-reduce(f32[8,1]{0,1:T(1,128)S(1)} %bitcast.75, f32[8,1]{0,1:T(1,128)S(1)} %bitcast.74, f32[8,1]{0,1:T(1,128)S(1)} %bitcast.77, f32[8,1]{0,1:T(1,128)S(1)} %bitcast.76), channel_id=1, replica_groups=mesh['ctg'=8,'br'=4] {'br'}, use_global_device_ids=true, to_apply=%region_13.14 | all-reduce | flops 32 | bytes 256 | tf_op jit(solution)/shard_map/psum | solution.py:146
  461.4 0.7 fusion.45
  462.1 11.8 %psum.39 = f32[4]{0:T(128)S(1)} all-reduce(f32[4]{0:T(128)S(1)} %get-tuple-element.188), channel_id=1, replica_groups=mesh['ctg'=8,'br'=4] {'ctg'}, use_global_device_ids=true, to_apply=%region_15.16 | all-reduce | flops 4 | bytes 32 | tf_op jit(solution)/shard_map/psum | solution.py:163
  (110 shorter events, 16.0 us)
Async XLA Ops:
  7.2 23.4 %copy-start.1 = (f32[8,2,2560]{2,1,0:T(2,128)S(1)}, f32[8,2,2560]{2,1,0:T(2,128)}, u32[]{:S(2)}) copy-start(f32[8,2,2560]{2,1,0:T(2,128)} %param.24) | copy-start | bytes 491524
  7.2 40.0 %copy-start.5 = (f32[3328]{0:T(1024)S(1)}, f32[3328]{0:T(1024)}, u32[]{:S(2)}) copy-start(f32[3328]{0:T(1024)} %param.31) | copy-start | bytes 39940
  7.2 40.0 %copy-start.11 = (f32[3328]{0:T(1024)S(1)}, f32[3328]{0:T(1024)}, u32[]{:S(2)}) copy-start(f32[3328]{0:T(1024)} %param.32) | copy-start | bytes 39940
  7.2 132.4 %all-reduce.6.cloned.1.call-start = ((), (), s32[]{:S(2)}) async-start(), calls=%async_computation.2 | async-start | bytes 163840
  7.3 40.0 %copy-start = (s32[8,3328]{1,0:T(8,128)S(1)}, s32[8,3328]{1,0:T(8,128)}, u32[]{:S(2)}) copy-start(s32[8,3328]{1,0:T(8,128)} %param.29) | copy-start | bytes 319492
  8.2 0.9 copy-start.4
  9.1 0.6 copy-start.3
  9.7 283.4 %all-gather.5.cloned.1.call-start = ((), (), s32[]{:S(2)}) async-start(), calls=%async_computation | async-start | bytes 1597440 | tf_op jit(solution)/shard_map/all_gather | solution.py:148
  47.2 94.2 %copy-start.13 = (s32[3328]{0:T(1024)S(1)}, s32[3328]{0:T(1024)}, u32[]{:S(2)}) copy-start(s32[3328]{0:T(1024)} %param.28) | copy-start | bytes 39940
  141.4 57.5 %copy-start.12 = (s32[3328]{0:T(1024)S(1)}, s32[3328]{0:T(1024)}, u32[]{:S(2)}) copy-start(s32[3328]{0:T(1024)} %param.27) | copy-start | bytes 39940
  198.9 57.5 %copy-start.9 = (f32[3328]{0:T(1024)S(1)}, f32[3328]{0:T(1024)}, u32[]{:S(2)}) copy-start(f32[3328]{0:T(1024)} %param.30) | copy-start | bytes 39940
  256.5 2.3 copy-start.10
  256.5 31.6 %copy-start.6 = (f32[8,3328]{1,0:T(8,128)S(1)}, f32[8,3328]{1,0:T(8,128)}, u32[]{:S(2)}) copy-start(f32[8,3328]{1,0:T(8,128)} %param.34) | copy-start | bytes 319492
  256.5 31.6 %copy-start.7 = (f32[8,3328]{1,0:T(8,128)S(1)}, f32[8,3328]{1,0:T(8,128)}, u32[]{:S(2)}) copy-start(f32[8,3328]{1,0:T(8,128)} %param.35) | copy-start | bytes 319492
  258.0 67.8 %all-gather.7.cloned.1.call-start = ((), (), s32[]{:S(2)}) async-start(), calls=%async_computation.1 | async-start | bytes 1597440 | tf_op jit(solution)/shard_map/all_gather | solution.py:149
  332.1 117.8 %copy-start.2 = (f32[8,2,2560]{2,1,0:T(2,128)S(1)}, f32[8,2,2560]{2,1,0:T(2,128)}, u32[]{:S(2)}) copy-start(f32[8,2,2560]{2,1,0:T(2,128)} %param.25) | copy-start | bytes 491524
  332.1 118.6 %copy-start.8 = (f32[8,2560]{1,0:T(8,128)S(1)}, f32[8,2560]{1,0:T(8,128)}, u32[]{:S(2)}) copy-start(f32[8,2560]{1,0:T(8,128)} %param.26) | copy-start | bytes 245764
Sparse Core Ops, SparseCore 0:
  14.2 125.3 all-reduce.5
  258.1 35.0 all-gather.4
  294.8 30.9 all-gather.6
where the time goes:
time: 482 us; the launch traced here: 481 us
  matrix products  193 us (40%)
  waiting for transfers between devices  129 us (27%)
  blocking collectives  87.4 us (18%)
  local copies, waits for them, and re-layouts  28.5 us (6%)
  loops' own time  20.3 us (4%)
  between operations  14.1 us (3%)
  other arithmetic  8.15 us (2%)
    dot_general x10, matrix products, one_block(): jnp.dot(values, onehot, precision=lax.Precision.HIGHEST, preferred_elemen...  104 us
    unnamed x4, waiting for transfers between devices  93.1 us
    dot_general x20, matrix products, add_block(): jnp.dot(segment, onehot, precision=lax.Precision.HIGHEST, preferred_eleme...  89.4 us
    all_gather x1, waiting for transfers between devices, per_device(): lax.all_gather(at_to, 'br', axis=2, tiled=True)  32.5 us
    all_gather x1, blocking collectives, per_device(): lax.all_gather(delta_state, 'br', axis=2, tiled=True)  19.8 us
    dynamic_slice x30, local copies, waits for them, and re-layouts, select_cols(): result, _ = lax.scan(add_block, start_zero, (tiles, numbers))  17.5 us
    all_gather x1, blocking collectives, per_device(): lax.all_gather(multipliers, 'br', axis=2, tiled=True)  16.5 us
    all_gather x1, blocking collectives, per_device(): lax.all_gather(from_bus, 'br', axis=0, tiled=True)  14.7 us
  transfers between devices with their start and end apart: 3, of which 3 were waited for; matrix products, arithmetic and copies ran while one was open for 1% of the time, Pallas kernels for 0%

commit v1 on v0

--- a/solution.py
+++ b/solution.py
@@ -146,7 +146,7 @@
     limit_sq, comp_sq = lax.psum((limit_part, comp_part), "br")
     every_from, every_to = (
         lax.all_gather(at_from, "br", axis=2, tiled=True),
-        lax.all_gather(at_to, "br", axis=2, tiled=True),
+        jnp.concatenate(lax.all_gather(at_to, "br"), axis=2),
     )
     ends_from, ends_to = (
         lax.all_gather(from_bus, "br", axis=0, tiled=True),

time: 482 us -> 473 us (0.981)
  matrix products: 193 us -> 187 us
    dot_general x10, matrix products: 104 us -> 97.9 us  [one_block(): jnp.dot(values, onehot, precision=lax.Precision.HIGHEST, preferred_elemen...]
where the time goes in v1:
time: 473 us; the launch traced here: 472 us
  matrix products  187 us (40%)
  waiting for transfers between devices  126 us (27%)
  blocking collectives  87.3 us (18%)
  local copies, waits for them, and re-layouts  28.4 us (6%)
  loops' own time  20.3 us (4%)
  between operations  14.1 us (3%)
  other arithmetic  7.7 us (2%)
    dot_general x10, matrix products, one_block(): jnp.dot(values, onehot, precision=lax.Precision.HIGHEST, preferred_elemen...  97.9 us
    unnamed x4, waiting for transfers between devices  92.4 us
    dot_general x20, matrix products, add_block(): jnp.dot(segment, onehot, precision=lax.Precision.HIGHEST, preferred_eleme...  89.5 us
    all_gather x1, waiting for transfers between devices, per_device(): lax.all_gather(at_to, 'br')  29.7 us
    all_gather x1, blocking collectives, per_device(): lax.all_gather(delta_state, 'br', axis=2, tiled=True)  19.8 us
    dynamic_slice x30, local copies, waits for them, and re-layouts, select_cols(): result, _ = lax.scan(add_block, start_zero, (tiles, numbers))  17.6 us
    all_gather x1, blocking collectives, per_device(): lax.all_gather(multipliers, 'br', axis=2, tiled=True)  16.5 us
    all_gather x1, blocking collectives, per_device(): lax.all_gather(from_bus, 'br', axis=0, tiled=True)  14.7 us
  transfers between devices with their start and end apart: 3, of which 3 were waited for; matrix products, arithmetic and copies ran while one was open for 1% of the time, Pallas kernels for 0%

profile of v1, /device:TPU:0, one launch (start us, length us, event | category | flops | bytes accessed | tf_op | source)
XLA Modules:
  0.0 471.5 jit_solution(5529265967075894320)
XLA Ops:
  7.2 0.9 dynamic-update-slice
  8.1 0.9 dynamic-update-slice.1
  9.0 0.6 copy-done.4
  9.7 1.0 copy.27
  10.7 19.8 %all_gather.28 = f32[8,2,10240]{2,0,1:T(8,128)S(1)} all-gather(f32[8,2,2560]{2,0,1:T(8,128)S(1)} %copy.27), channel_id=1, replica_groups=mesh['ctg'=8,'br'=4] {'br'}, dimensions={2}, use_global_device_ids=true | all-gather | bytes 819200 | tf_op jit(solution)/shard_map/all_gather | solution.py:120
  30.6 16.5 %all_gather.30 = f32[8,2,10240]{2,0,1:T(8,128)S(1)} all-gather(f32[8,2,2560]{2,0,1:T(8,128)S(1)} %copy.28), channel_id=1, replica_groups=mesh['ctg'=8,'br'=4] {'br'}, dimensions={2}, use_global_device_ids=true | all-gather | bytes 819200 | tf_op jit(solution)/shard_map/all_gather | solution.py:121
  47.2 92.3 %all-reduce.6.cloned.1.call-done = (f32[10240]{0:T(1024)}, f32[10240]{0:T(1024)}) async-done(((f32[10240]{0:T(1024)}, f32[10240]{0:T(1024)}), (f32[10240]{0:T(1024)}, f32[10240]{0:T(1024)})) %all-reduce.6.cloned.1.call-update) | async-done | bytes 81936
  139.5 0.8 add.111
  140.3 0.8 add.114
  141.8 57.5 %while.34 = (s32[]{:T(128)}, f32[32,3328]{1,0:T(8,128)S(1)}, f32[10,32,1024]{2,1,0:T(8,128)S(1)}, s32[10]{0:T(128)S(1)}, s32[3328]{0:T(1024)S(1)}, /*index=5*/s32[]{:T(128)}, s32[1]{0:T(128)}, s32[]{:T(128)}) while((s32[]{:T(128)}, f32[32,3328]{1,0:T(8,128)S(1)}, f32[10,32,1024]{2,1,0:T(8,128)S(1)}, s32[10]{0:T(128)S(1)}, ...), condition=%wide.region_3.4_spmd.clone, body=%wide.region_2.3_spmd.clone.sunk | while | flops 1312244736 | bytes 1007743 | solution.py:32
  143.1 4.5 fusion.70
  148.8 4.5 fusion.70
  154.6 4.5 fusion.70
  160.3 4.5 fusion.70
  166.1 4.5 fusion.70
  171.8 4.5 fusion.70
  177.6 4.5 fusion.70
  183.3 4.5 fusion.70
  189.1 4.5 fusion.70
  194.8 4.5 fusion.70
  199.3 57.5 %while.33 = (s32[]{:T(128)}, f32[32,3328]{1,0:T(8,128)S(1)}, f32[10,32,1024]{2,1,0:T(8,128)S(1)}, s32[10]{0:T(128)S(1)}, s32[3328]{0:T(1024)S(1)}, /*index=5*/s32[]{:T(128)}, s32[1]{0:T(128)}, s32[]{:T(128)}) while((s32[]{:T(128)}, f32[32,3328]{1,0:T(8,128)S(1)}, f32[10,32,1024]{2,1,0:T(8,128)S(1)}, s32[10]{0:T(128)S(1)}, ...), condition=%wide.region_1.2_spmd.clone, body=%wide.region_0.1_spmd.clone.sunk | while | flops 1312244736 | bytes 1007743 | solution.py:32
  200.6 4.5 fusion.67
  206.4 4.5 fusion.67
  212.1 4.5 fusion.67
  217.9 4.5 fusion.67
  223.6 4.5 fusion.67
  229.4 4.5 fusion.67
  235.1 4.5 fusion.67
  240.9 4.5 fusion.67
  246.6 4.5 fusion.67
  252.4 4.5 fusion.67
  257.5 0.8 maximum_multiply_fusion
  258.3 0.8 maximum_multiply_fusion.1
  259.2 14.7 %all-gather = s32[4,1,3328]{2,1,0:T(1,128)S(1)} all-gather(s32[1,1,3328]{2,1,0:T(1,128)S(1)} %reshape.119), channel_id=1, replica_groups=mesh['ctg'=8,'br'=4] {'br'}, dimensions={0}, use_global_device_ids=true | all-gather | bytes 66560 | tf_op jit(solution)/shard_map/all_gather | solution.py:152
  273.9 14.5 %all-gather.1 = s32[4,1,3328]{2,1,0:T(1,128)S(1)} all-gather(s32[1,1,3328]{2,1,0:T(1,128)S(1)} %reshape.121), channel_id=1, replica_groups=mesh['ctg'=8,'br'=4] {'br'}, dimensions={0}, use_global_device_ids=true | all-gather | bytes 66560 | tf_op jit(solution)/shard_map/all_gather | solution.py:153
  288.5 0.8 multiply_reduce_fusion.2
  289.3 4.1 all-gather.5.cloned.1.call-done
  293.5 2.2 copy.29
  295.7 0.6 concatenate.30
  296.3 29.7 %all-gather.7.cloned.1.call-done = f32[4,8,3,3328]{3,1,2,0:T(8,128)} async-done(((f32[1,8,3,3328]{3,1,2,0:T(8,128)}), f32[4,8,3,3328]{3,1,2,0:T(8,128)}) %all-gather.7.cloned.1.call-update) | async-done | bytes 1277968 | tf_op jit(solution)/shard_map/all_gather | solution.py:149
  326.0 1.8 copy.30
  328.1 1.7 pad_maximum_fusion
  329.7 110.4 %while.32 = (s32[]{:T(128)}, f32[10,24,256]{2,1,0:T(8,128)S(1)}, s32[26624]{0:T(1024)S(1)}, s32[10]{0:T(128)S(1)}, f32[24,26624]{1,0:T(8,128)}, /*index=5*/s32[]{:T(128)}, s32[1]{0:T(128)}) while((s32[]{:T(128)}, f32[10,24,256]{2,1,0:T(8,128)S(1)}, s32[26624]{0:T(1024)S(1)}, s32[10]{0:T(128)S(1)}, f32[24,26624]{1,0:T(8,128)}, ...), condition=%wide.region_5.6_spmd, body=%wide.region_4.5_spmd.sunk | while | flops 1969750272 | bytes 2689133 | solution.py:50
  331.0 9.8 %fusion.64 = f32[10,24,256]{2,1,0:T(8,128)S(1)} fusion(f32[10,24,256]{2,1,0:T(8,128)S(1)} %get-tuple-element.339, s32[]{:T(128)} %get-tuple-element.338, f32[24,26624]{1,0:T(8,128)} %get-tuple-element.349, s32[256]{0:T(256)S(1)} %iota_add_fusion.6, s32[26624]{0:T(1024)S(1)} %get-tuple-element.347), kind=kOutput, calls=%fused_computation.5.clone.1 | convolution fusion | flops 1969750016 | bytes 2688004 | tf_op jit(solution)/shard_map/while/body/eval_jaxpr/dot_general | solution.py:44
  340.8 0.6 dynamic_slice.34
  342.0 9.8 %fusion.64 = f32[10,24,256]{2,1,0:T(8,128)S(1)} fusion(f32[10,24,256]{2,1,0:T(8,128)S(1)} %get-tuple-element.339, s32[]{:T(128)} %get-tuple-element.338, f32[24,26624]{1,0:T(8,128)} %get-tuple-element.349, s32[256]{0:T(256)S(1)} %iota_add_fusion.6, s32[26624]{0:T(1024)S(1)} %get-tuple-element.347), kind=kOutput, calls=%fused_computation.5.clone.1 | convolution fusion | flops 1969750016 | bytes 2688004 | tf_op jit(solution)/shard_map/while/body/eval_jaxpr/dot_general | solution.py:44
  351.8 0.6 dynamic_slice.34
  353.1 9.8 %fusion.64 = f32[10,24,256]{2,1,0:T(8,128)S(1)} fusion(f32[10,24,256]{2,1,0:T(8,128)S(1)} %get-tuple-element.339, s32[]{:T(128)} %get-tuple-element.338, f32[24,26624]{1,0:T(8,128)} %get-tuple-element.349, s32[256]{0:T(256)S(1)} %iota_add_fusion.6, s32[26624]{0:T(1024)S(1)} %get-tuple-element.347), kind=kOutput, calls=%fused_computation.5.clone.1 | convolution fusion | flops 1969750016 | bytes 2688004 | tf_op jit(solution)/shard_map/while/body/eval_jaxpr/dot_general | solution.py:44
  362.8 0.6 dynamic_slice.34
  364.1 9.8 %fusion.64 = f32[10,24,256]{2,1,0:T(8,128)S(1)} fusion(f32[10,24,256]{2,1,0:T(8,128)S(1)} %get-tuple-element.339, s32[]{:T(128)} %get-tuple-element.338, f32[24,26624]{1,0:T(8,128)} %get-tuple-element.349, s32[256]{0:T(256)S(1)} %iota_add_fusion.6, s32[26624]{0:T(1024)S(1)} %get-tuple-element.347), kind=kOutput, calls=%fused_computation.5.clone.1 | convolution fusion | flops 1969750016 | bytes 2688004 | tf_op jit(solution)/shard_map/while/body/eval_jaxpr/dot_general | solution.py:44
  373.9 0.6 dynamic_slice.34
  375.1 9.8 %fusion.64 = f32[10,24,256]{2,1,0:T(8,128)S(1)} fusion(f32[10,24,256]{2,1,0:T(8,128)S(1)} %get-tuple-element.339, s32[]{:T(128)} %get-tuple-element.338, f32[24,26624]{1,0:T(8,128)} %get-tuple-element.349, s32[256]{0:T(256)S(1)} %iota_add_fusion.6, s32[26624]{0:T(1024)S(1)} %get-tuple-element.347), kind=kOutput, calls=%fused_computation.5.clone.1 | convolution fusion | flops 1969750016 | bytes 2688004 | tf_op jit(solution)/shard_map/while/body/eval_jaxpr/dot_general | solution.py:44
  384.9 0.6 dynamic_slice.34
  386.2 9.8 %fusion.64 = f32[10,24,256]{2,1,0:T(8,128)S(1)} fusion(f32[10,24,256]{2,1,0:T(8,128)S(1)} %get-tuple-element.339, s32[]{:T(128)} %get-tuple-element.338, f32[24,26624]{1,0:T(8,128)} %get-tuple-element.349, s32[256]{0:T(256)S(1)} %iota_add_fusion.6, s32[26624]{0:T(1024)S(1)} %get-tuple-element.347), kind=kOutput, calls=%fused_computation.5.clone.1 | convolution fusion | flops 1969750016 | bytes 2688004 | tf_op jit(solution)/shard_map/while/body/eval_jaxpr/dot_general | solution.py:44
  397.2 9.8 %fusion.64 = f32[10,24,256]{2,1,0:T(8,128)S(1)} fusion(f32[10,24,256]{2,1,0:T(8,128)S(1)} %get-tuple-element.339, s32[]{:T(128)} %get-tuple-element.338, f32[24,26624]{1,0:T(8,128)} %get-tuple-element.349, s32[256]{0:T(256)S(1)} %iota_add_fusion.6, s32[26624]{0:T(1024)S(1)} %get-tuple-element.347), kind=kOutput, calls=%fused_computation.5.clone.1 | convolution fusion | flops 1969750016 | bytes 2688004 | tf_op jit(solution)/shard_map/while/body/eval_jaxpr/dot_general | solution.py:44
  407.0 0.6 dynamic_slice.34
  408.3 9.8 %fusion.64 = f32[10,24,256]{2,1,0:T(8,128)S(1)} fusion(f32[10,24,256]{2,1,0:T(8,128)S(1)} %get-tuple-element.339, s32[]{:T(128)} %get-tuple-element.338, f32[24,26624]{1,0:T(8,128)} %get-tuple-element.349, s32[256]{0:T(256)S(1)} %iota_add_fusion.6, s32[26624]{0:T(1024)S(1)} %get-tuple-element.347), kind=kOutput, calls=%fused_computation.5.clone.1 | convolution fusion | flops 1969750016 | bytes 2688004 | tf_op jit(solution)/shard_map/while/body/eval_jaxpr/dot_general | solution.py:44
  419.3 9.8 %fusion.64 = f32[10,24,256]{2,1,0:T(8,128)S(1)} fusion(f32[10,24,256]{2,1,0:T(8,128)S(1)} %get-tuple-element.339, s32[]{:T(128)} %get-tuple-element.338, f32[24,26624]{1,0:T(8,128)} %get-tuple-element.349, s32[256]{0:T(256)S(1)} %iota_add_fusion.6, s32[26624]{0:T(1024)S(1)} %get-tuple-element.347), kind=kOutput, calls=%fused_computation.5.clone.1 | convolution fusion | flops 1969750016 | bytes 2688004 | tf_op jit(solution)/shard_map/while/body/eval_jaxpr/dot_general | solution.py:44
  430.3 9.8 %fusion.64 = f32[10,24,256]{2,1,0:T(8,128)S(1)} fusion(f32[10,24,256]{2,1,0:T(8,128)S(1)} %get-tuple-element.339, s32[]{:T(128)} %get-tuple-element.338, f32[24,26624]{1,0:T(8,128)} %get-tuple-element.349, s32[256]{0:T(256)S(1)} %iota_add_fusion.6, s32[26624]{0:T(1024)S(1)} %get-tuple-element.347), kind=kOutput, calls=%fused_computation.5.clone.1 | convolution fusion | flops 1969750016 | bytes 2688004 | tf_op jit(solution)/shard_map/while/body/eval_jaxpr/dot_general | solution.py:44
  440.5 0.8 multiply_reduce_fusion
  441.3 0.8 multiply_reduce_fusion.3
  442.0 10.0 %all-reduce.3 = (f32[8,1]{0,1:T(1,128)S(1)}, f32[8,1]{0,1:T(1,128)S(1)}, f32[8,1]{0,1:T(1,128)S(1)}, f32[8,1]{0,1:T(1,128)S(1)}) all-reduce(f32[8,1]{0,1:T(1,128)S(1)} %bitcast.82, f32[8,1]{0,1:T(1,128)S(1)} %bitcast.81, f32[8,1]{0,1:T(1,128)S(1)} %bitcast.84, f32[8,1]{0,1:T(1,128)S(1)} %bitcast.83), channel_id=1, replica_groups=mesh['ctg'=8,'br'=4] {'br'}, use_global_device_ids=true, to_apply=%region_13.14 | all-reduce | flops 32 | bytes 256 | tf_op jit(solution)/shard_map/psum | solution.py:146
  452.0 0.7 fusion.45
  452.7 11.8 %psum.39 = f32[4]{0:T(128)S(1)} all-reduce(f32[4]{0:T(128)S(1)} %get-tuple-element.186), channel_id=1, replica_groups=mesh['ctg'=8,'br'=4] {'ctg'}, use_global_device_ids=true, to_apply=%region_15.16 | all-reduce | flops 4 | bytes 32 | tf_op jit(solution)/shard_map/psum | solution.py:163
  (115 shorter events, 16.9 us)
Async XLA Ops:
  7.2 23.4 %copy-start.2 = (f32[8,2,2560]{2,1,0:T(2,128)S(1)}, f32[8,2,2560]{2,1,0:T(2,128)}, u32[]{:S(2)}) copy-start(f32[8,2,2560]{2,1,0:T(2,128)} %param.24) | copy-start | bytes 491524
  7.2 132.3 %all-reduce.6.cloned.1.call-start = ((), (), s32[]{:S(2)}) async-start(), calls=%async_computation.2 | async-start | bytes 163840
  8.1 0.9 copy-start.5
  9.0 0.6 copy-start.4
  9.7 283.8 %all-gather.5.cloned.1.call-start = ((), (), s32[]{:S(2)}) async-start(), calls=%async_computation | async-start | bytes 1597440 | tf_op jit(solution)/shard_map/all_gather | solution.py:148
  30.5 16.6 %copy-start.6 = (f32[3328]{0:T(1024)S(1)}, f32[3328]{0:T(1024)}, u32[]{:S(2)}) copy-start(f32[3328]{0:T(1024)} %param.31) | copy-start | bytes 39940
  30.5 16.6 %copy-start.12 = (f32[3328]{0:T(1024)S(1)}, f32[3328]{0:T(1024)}, u32[]{:S(2)}) copy-start(f32[3328]{0:T(1024)} %param.32) | copy-start | bytes 39940
  30.5 16.7 %copy-start.1 = (s32[8,3328]{1,0:T(8,128)S(1)}, s32[8,3328]{1,0:T(8,128)}, u32[]{:S(2)}) copy-start(s32[8,3328]{1,0:T(8,128)} %param.29) | copy-start | bytes 319492
  141.1 0.7 copy-start.14
  141.8 57.5 %copy-start.13 = (s32[3328]{0:T(1024)S(1)}, s32[3328]{0:T(1024)}, u32[]{:S(2)}) copy-start(s32[3328]{0:T(1024)} %param.27) | copy-start | bytes 39940
  199.3 57.5 %copy-start.10 = (f32[3328]{0:T(1024)S(1)}, f32[3328]{0:T(1024)}, u32[]{:S(2)}) copy-start(f32[3328]{0:T(1024)} %param.30) | copy-start | bytes 39940
  257.3 1.8 copy-start.11
  257.3 31.2 %copy-start.7 = (f32[8,3328]{1,0:T(8,128)S(1)}, f32[8,3328]{1,0:T(8,128)}, u32[]{:S(2)}) copy-start(f32[8,3328]{1,0:T(8,128)} %param.34) | copy-start | bytes 319492
  257.3 31.2 %copy-start.8 = (f32[8,3328]{1,0:T(8,128)S(1)}, f32[8,3328]{1,0:T(8,128)}, u32[]{:S(2)}) copy-start(f32[8,3328]{1,0:T(8,128)} %param.35) | copy-start | bytes 319492
  258.2 30.3 %copy-start = (f32[8,3,3328]{2,0,1:T(8,128)S(1)}, f32[8,3,3328]{2,0,1:T(8,128)}, u32[]{:S(2)}) copy-start(f32[8,3,3328]{2,0,1:T(8,128)} %maximum_multiply_fusion) | copy-start | bytes 958468
  258.2 67.8 %all-gather.7.cloned.1.call-start = ((), (), s32[]{:S(2)}) async-start(), calls=%async_computation.1 | async-start | bytes 1597440 | tf_op jit(solution)/shard_map/all_gather | solution.py:149
  329.7 110.8 %copy-start.3 = (f32[8,2,2560]{2,1,0:T(2,128)S(1)}, f32[8,2,2560]{2,1,0:T(2,128)}, u32[]{:S(2)}) copy-start(f32[8,2,2560]{2,1,0:T(2,128)} %param.25) | copy-start | bytes 491524
  440.1 1.1 copy-start.9
Sparse Core Ops, SparseCore 0:
  14.2 125.2 all-reduce.5
  258.4 35.0 all-gather.4
  295.1 30.9 all-gather.6
